TPU v7x, 128 devices: a whole 4x4x4 slice. The times are simulated.
128 devices in a mesh: fsdp: 16 (over y, x_hi, core), tp: 8 (over z, x_lo).
Axes of the slice: x: 4 (x_hi: 2, x_lo: 2; x = x_hi * 2 + x_lo), y: 4, z: 4, core: 2. Of those that a mesh axis runs over, the one named last changes fastest.
Arguments:
- w_gate: float32 [3072, 8192], P('fsdp', 'tp'), may hold values from -0.15625 to 0.15625
- first_gate: float32 [3072, 8192], P('fsdp', 'tp'), may hold values from -0.109375 to 0.109375
- second_gate: float32 [3072, 8192], P('fsdp', 'tp'), may hold values from -0.109375 to 0.109375
- w_up: float32 [3072, 8192], P('fsdp', 'tp'), may hold values from -0.15625 to 0.15625
- first_up: float32 [3072, 8192], P('fsdp', 'tp'), may hold values from -0.109375 to 0.109375
- second_up: float32 [3072, 8192], P('fsdp', 'tp'), may hold values from -0.109375 to 0.109375
- norm_train: float32 [3072], P(('fsdp', 'tp')), may hold values from 0.25 to 1.75
- norm_step: float32 [3072], P(('fsdp', 'tp')), may hold values from -0.3 to 0.3
Outputs:
- serving_gate: bfloat16 [3072, 8192], P(None, 'tp')
- serving_up: bfloat16 [3072, 8192], P(None, 'tp')
- scale_gate: float32 [8192], P('tp')
- scale_up: float32 [8192], P('tp')
- serve_norm: bfloat16 [3072], replicated
- whole_gate: float32 [3072, 8192], P('fsdp', 'tp')
- whole_up: float32 [3072, 8192], P('fsdp', 'tp')
All inputs are finite; a program needn't handle non-finite values. Where the computation divides by a largest or mean magnitude, that divisor is 1e-20 or more.
Results may differ from a plain program's by a relative error of at most 0.001.
Values may be sent and summed in bfloat16 or wider, within the bound.
A program may use at most 128 MiB of HBM per device.

v0:
```python
import jax
import jax.numpy as jnp
from jax import lax
from jax.sharding import PartitionSpec as P

D_MODEL = 3072


learn_rate = 0.25
hold_rate = 0.9


def from_everyone(shard, axis):
    length = lax.axis_size(axis)
    return lax.all_to_all(
        jnp.broadcast_to(shard[None], (length, *shard.shape)), axis, 0, 0, tiled=True
    )


def of_everyone(shard, axis):
    everything = from_everyone(shard, axis)
    return jnp.sum(everything, axis=0)


def together(arrays, axis):
    flat, at, gathered = (jnp.concatenate([a.reshape(-1) for a in arrays]), 0, [])
    so_far = of_everyone(flat, axis)
    for a in arrays:
        gathered.append(so_far[at : at + a.size].reshape(a.shape))
        at += a.size
    return tuple(gathered)


def sent_together(arrays, axis, dim, along):
    ends, at = ([], 0)
    for a in arrays[:-1]:
        at += a.shape[along]
        ends.append(at)
    both = jnp.concatenate(arrays, axis=along)
    return tuple(jnp.split(lax.all_gather(both, axis, axis=dim, tiled=True), ends, axis=along))


def per_device(w_gate, first_gate, second_gate, w_up, first_up, second_up, norm_train, norm_step):
    hold_gate = hold_rate * first_gate + second_gate
    whole_gate = w_gate - learn_rate * hold_gate
    hold_up = hold_rate * first_up + second_up
    whole_up = w_up - learn_rate * hold_up
    total_gate, total_up = together(
        (jnp.sum(jnp.abs(whole_gate), axis=0), jnp.sum(jnp.abs(whole_up), axis=0)), "fsdp"
    )
    scale_gate = total_gate / D_MODEL
    scale_up = total_up / D_MODEL
    narrow_gate, narrow_up = (
        (whole_gate / scale_gate).astype(jnp.bfloat16),
        (whole_up / scale_up).astype(jnp.bfloat16),
    )
    serving_gate, serving_up = sent_together((narrow_gate, narrow_up), "fsdp", 0, 1)
    serve_norm = lax.all_gather(
        (norm_train + norm_step).astype(jnp.bfloat16), ("fsdp", "tp"), axis=0, tiled=True
    )
    return (serving_gate, serving_up, scale_gate, scale_up, serve_norm, whole_gate, whole_up)


def solution(mesh):
    return jax.shard_map(
        per_device,
        mesh=mesh,
        in_specs=(
            P("fsdp", "tp"),
            P("fsdp", "tp"),
            P("fsdp", "tp"),
            P("fsdp", "tp"),
            P("fsdp", "tp"),
            P("fsdp", "tp"),
            P(("fsdp", "tp")),
            P(("fsdp", "tp")),
        ),
        out_specs=(
            P(None, "tp"),
            P(None, "tp"),
            P("tp"),
            P("tp"),
            P(),
            P("fsdp", "tp"),
            P("fsdp", "tp"),
        ),
        check_vma=False,
    )
```

profile of v0, /device:TPU:1, one launch (start us, length us, event | category | flops | bytes accessed | tf_op | source)
XLA Modules:
  0.0 144.8 jit_solution(7183438300629721995)
XLA Ops:
  7.2 0.0 copy-start.4
  7.2 0.0 copy-start.5
  7.2 0.0 all-gather.2.cloned.1.call-start
  7.2 2.9 %abs_reduce_fusion = (f32[1024]{0:T(1024)S(1)}, f32[192,1024]{1,0:T(8,128)S(1)}, f32[1024]{0:T(1024)S(1)}, f32[192,1024]{1,0:T(8,128)S(1)}) fusion(f32[192,1024]{1,0:T(8,128)} %param.11, f32[192,1024]{1,0:T(8,128)} %param.13, f32[192,1024]{1,0:T(8,128)} %param.12, f32[192,1024]{1,0:T(8,128)} %param.8, f32[192,1024]{1,0:T(8,128)} %param.10, f32[192,1024]{1,0:T(8,128)} %param.9), kind=kLoop, calls=%fused_computation.3 | loop fusion | flops 2357248 | bytes 6299648 | tf_op jit(solution)/shard_map/reduce_sum | solution.py:49
  10.1 0.0 copy-start
  10.1 0.0 copy-start.1
  10.1 0.1 broadcast_in_dim.2
  10.2 15.8 %all_to_all.6 = f32[16,1,2048]{2,1,0:T(1,128)S(1)} all-to-all(f32[16,1,2048]{2,1,0:T(1,128)S(1)} %broadcast_in_dim.2), channel_id=1, replica_groups=mesh['fsdp'=16,'tp'=8] {'fsdp'}, dimensions={0} | all-to-all | bytes 262144 | tf_op jit(solution)/shard_map/all_to_all | solution.py:15
  26.1 0.1 reduce_sum.29
  26.2 0.0 copy-start.2
  26.2 0.0 copy-start.3
  26.2 0.1 divide_convert_fusion.1
  26.3 0.1 divide_convert_fusion
  26.4 0.9 pad_maximum_fusion
  27.3 0.0 all-gather.2.cloned.1.call-update
  27.3 0.0 copy-done.4
  27.3 0.0 copy-done.5
  27.4 0.2 dynamic-update-slice
  27.6 99.9 %all-reduce = bf16[3072]{0:T(1024)(128)(2,1)} all-reduce(bf16[3072]{0:T(1024)(128)(2,1)S(1)} %dynamic-update-slice), channel_id=1, replica_groups=mesh['fsdp'=16,'tp'=8] {'fsdp','tp'}, use_global_device_ids=true, to_apply=%add | all-reduce | flops 3072 | bytes 12288
  127.5 0.0 all-gather.2.cloned.1.call-done
  127.5 10.4 %fusion = (bf16[3072,1024]{1,0:T(8,128)(2,1)}, bf16[3072,1024]{1,0:T(8,128)(2,1)}) fusion(bf16[3072,2048]{1,0:T(8,128)(2,1)} %all-gather.2.cloned.1.call-done), kind=kLoop, calls=%fused_computation.11 | loop fusion | bytes 25165824 | tf_op jit(solution)/shard_map/split | solution.py:40
  137.9 0.0 copy-done
  137.9 0.0 copy-done.1
  137.9 0.0 copy-done.2
  137.9 0.0 copy-done.3
  (4 shorter events, 0.0 us)
Async XLA Ops:
  7.2 20.2 %copy-start.4 = (f32[24]{0:T(128)S(1)}, f32[24]{0:T(128)}, u32[]{:S(2)}) copy-start(f32[24]{0:T(128)} %param.14) | copy-start | bytes 292
  7.2 20.2 %copy-start.5 = (f32[24]{0:T(128)S(1)}, f32[24]{0:T(128)}, u32[]{:S(2)}) copy-start(f32[24]{0:T(128)} %param.15) | copy-start | bytes 292
  7.2 120.3 %all-gather.2.cloned.1.call-start = ((), (), s32[]{:S(2)}) async-start(), calls=%async_computation.1 | async-start | bytes 13369344 | tf_op jit(solution)/shard_map/all_gather | solution.py:40
  10.1 127.8 %copy-start = (f32[192,1024]{1,0:T(8,128)}, f32[192,1024]{1,0:T(8,128)S(1)}, u32[]{:S(2)}) copy-start(f32[192,1024]{1,0:T(8,128)S(1)} %get-tuple-element.10) | copy-start | bytes 2359300
  10.1 127.8 %copy-start.1 = (f32[192,1024]{1,0:T(8,128)}, f32[192,1024]{1,0:T(8,128)S(1)}, u32[]{:S(2)}) copy-start(f32[192,1024]{1,0:T(8,128)S(1)} %get-tuple-element.16) | copy-start | bytes 2359300
  26.2 111.7 %copy-start.2 = (f32[1024]{0:T(1024)}, f32[1024]{0:T(1024)S(1)}, u32[]{:S(2)}) copy-start(f32[1024]{0:T(1024)S(1)} %get-tuple-element.13) | copy-start | bytes 12292
  26.2 111.7 %copy-start.3 = (f32[1024]{0:T(1024)}, f32[1024]{0:T(1024)S(1)}, u32[]{:S(2)}) copy-start(f32[1024]{0:T(1024)S(1)} %get-tuple-element.14) | copy-start | bytes 12292
Sparse Core Ops, SparseCore 0:
  27.4 89.0 all-gather.1
where the time goes:
time: 145 us
  blocking collectives  116 us (80%)
  between operations  14.2 us (10%)
  local copies, waits for them, and re-layouts  10.8 us (7%)
  other arithmetic  4.05 us (3%)
    unnamed x1, blocking collectives  99.9 us
    all_to_all x1, blocking collectives, from_everyone(): lax.all_to_all(jnp.broadcast_to(shard[None], (length, *shard.shape)), axi...  15.8 us
    split x1, local copies, waits for them, and re-layouts, sent_together(): jnp.split(lax.all_gather(both, axis, axis=dim, tiled=True), ends, axis=al...  10.4 us
  transfers between devices with their start and end apart: 1, of which 0 were waited for; matrix products, arithmetic and copies ran while one was open for 0% of the time, Pallas kernels for 0%

commit v1 on v0

v1 whole, which is shorter than its diff:
```python
import functools

import jax
import jax.numpy as jnp
from jax import lax
from jax.experimental import pallas as pl
from jax.experimental.pallas import tpu as pltpu
from jax.sharding import PartitionSpec as P

MESH = pl.DeviceIdType.MESH
LEARN_RATE = 0.25
HOLD_RATE = 0.9

UNITS = ((0, 64, 1, False), (96, 64, -1, False), (64, 32, 1, True), (160, 32, -1, True))
A, B, C, D, E, F, G = range(7)


def kernel(
    d_model, wg, fg, sg, wu, fu, su, nt, ns,
    serve_g, serve_u, scale_g, scale_u, norm_out, whole_g, whole_u,
    a1, a2, b1, b2, n0, n1, part, own_norm, near, far, norm,
    in_sem, tree_send, tree_recv, part_send, part_recv, norm_send, norm_recv, d2d_send, d2d_recv,
):
    f, t = lax.axis_index("fsdp"), lax.axis_index("tp")
    y, p, c = f // 4, (f // 2) % 2, f % 2

    def at(dy, dp, dc):
        return ((y + dy + 4) % 4) * 4 + ((p + dp) % 2) * 2 + (c + dc) % 2

    peers = [at(dy, dp, dc) for dy in (2, 1, 3, 0) for dp in (1, 0) for dc in (1, 0) if (dy, dp, dc) != (0, 0, 0)]
    peers_tp = [(t + k) % 8 for k in range(1, 8)]

    barrier = pltpu.get_barrier_semaphore()
    for q in peers:
        pl.semaphore_signal(barrier, inc=1, device_id=(q, t), device_id_type=MESH)
    for q in peers_tp:
        pl.semaphore_signal(barrier, inc=1, device_id=(f, q), device_id_type=MESH)

    serve, scale = (serve_g, serve_u), (scale_g, scale_u)
    pairs = ((wg, whole_g), (fg, a1), (sg, a2), (wu, whole_u), (fu, b1), (su, b2), (nt, n0), (ns, n1))
    loads = [pltpu.make_async_copy(src, dst, in_sem.at[i]) for i, (src, dst) in enumerate(pairs)]
    for load in loads:
        load.start()

    def remote(src, dst, send, recv, q):
        return pltpu.make_async_remote_copy(
            src_ref=src, dst_ref=dst, send_sem=send, recv_sem=recv, device_id=(q, t), device_id_type=MESH
        )

    def update(g, w, m1, m2):
        whole = w[...] - LEARN_RATE * (HOLD_RATE * m1[...] + m2[...])
        w[...] = whole
        part[g, f] = jnp.sum(jnp.abs(whole), axis=0, keepdims=True)

    def share(g):
        for q in peers:
            remote(part.at[g, f], part.at[g, f], part_send.at[g], part_recv.at[g], q).start()

    def narrow(g, w):
        pltpu.make_async_copy(part.at[g, pl.ds(0, 15)], part.at[g, pl.ds(0, 15)], part_recv.at[g]).wait()
        mean = jnp.sum(part[g], axis=0) / d_model
        scale[g][...] = mean
        serve[g][f] = (w[...] * (1.0 / mean)).astype(jnp.bfloat16)

    def rows(g, u, block):
        return serve[g].at[block, pl.ds(UNITS[u][0], UNITS[u][1])]

    late = []

    def send(g, u, kind, block, q):
        cp = remote(rows(g, u, block), rows(g, u, block), tree_send.at[g, u, kind], tree_recv.at[g, u, kind], q)
        cp.start()
        late.append(cp.wait_send)

    def arrived(g, u, kind, block):
        remote(rows(g, u, block), rows(g, u, block), tree_send.at[g, u, kind], tree_recv.at[g, u, kind], f).wait_recv()

    given = []

    def swap(g, dy, dp):
        block, k = at(dy, dp, 0), dy * 2 + dp
        return remote(serve[g].at[block], serve[g].at[block], d2d_send.at[g, k], d2d_recv.at[g, k], at(0, 0, 1))

    def give(g, dy, dp):
        cp = swap(g, dy, dp)
        cp.start()
        late.append(cp.wait_send)
        given.append((g, dy, dp))

    def take():
        g, dy, dp = given.pop(0)
        block, k = at(dy, dp, 1), dy * 2 + dp
        remote(serve[g].at[block], serve[g].at[block], d2d_send.at[g, k], d2d_recv.at[g, k], f).wait_recv()

    def own(g):
        for u, (_, _, s, _) in enumerate(UNITS):
            send(g, u, A, f, at(s, 0, 0))
            send(g, u, C, f, at(0, 1, 0))
            send(g, u, B, f, at(-s, 0, 0))

    for load in loads[:3]:
        load.wait()
    update(0, whole_g, a1, a2)
    pl.semaphore_wait(barrier, len(peers) + len(peers_tp))
    share(0)
    for load in loads[3:6]:
        load.wait()
    update(1, whole_u, b1, b2)
    share(1)
    narrow(0, whole_g)
    own(0)
    narrow(1, whole_u)
    own(1)

    for load in loads[6:]:
        load.wait()
    own_norm[...] = jnp.zeros_like(own_norm)
    own_norm[0:1, 0:24] = (n0[...] + n1[...]).astype(jnp.bfloat16).astype(jnp.float32)
    first = 24 * t + 64 * (f % 2)
    rolled = pltpu.roll(jnp.broadcast_to(own_norm[0:1, :], (8, 128)), first % 128, 1)
    place = 128 * lax.broadcasted_iota(jnp.int32, (8, 128), 0) + lax.broadcasted_iota(jnp.int32, (8, 128), 1) - first
    near[t] = jnp.where((place >= 0) & (place < 24), rolled, 0.0)
    for q in peers_tp:
        pltpu.make_async_remote_copy(
            src_ref=near.at[t], dst_ref=near.at[t], send_sem=norm_send.at[0], recv_sem=norm_recv.at[0],
            device_id=(f, q), device_id_type=MESH,
        ).start()

    for g in (0, 1):
        give(g, 0, 0)

    for g in (0, 1):
        for u, (_, _, s, three) in enumerate(UNITS):
            arrived(g, u, A, at(-s, 0, 0))
            send(g, u, D, at(-s, 0, 0), at(s, 0, 0))
            send(g, u, E, at(-s, 0, 0), at(0, 1, 0))
            arrived(g, u, C, at(0, 1, 0))
            if not three:
                send(g, u, F, at(0, 1, 0), at(-s, 0, 0))
        give(g, 0, 1)
        take()
        if g == 0:
            pltpu.make_async_copy(near.at[pl.ds(0, 7)], near.at[pl.ds(0, 7)], norm_recv.at[0]).wait()
            far[f] = jnp.sum(near[...], axis=0)
            for q in peers:
                remote(far.at[f], far.at[f], norm_send.at[1], norm_recv.at[1], q).start()
    for g in (0, 1):
        for u, (_, _, s, three) in enumerate(UNITS):
            arrived(g, u, B, at(s, 0, 0))
            if three:
                send(g, u, F, at(s, 0, 0), at(0, 1, 0))
        give(g, 1, 0)
        give(g, 3, 0)
        take()
    for g in (0, 1):
        for u, (_, _, s, _) in enumerate(UNITS):
            arrived(g, u, E, at(-s, 1, 0))
            send(g, u, G, at(-s, 1, 0), at(s, 0, 0))
        take()
    for g in (0, 1):
        for u in range(len(UNITS)):
            arrived(g, u, D, at(2, 0, 0))
        give(g, 2, 0)
        take()

    pltpu.make_async_copy(far.at[pl.ds(0, 15)], far.at[pl.ds(0, 15)], norm_recv.at[1]).wait()
    norm[...] = jnp.zeros_like(norm)
    for i in range(16):
        r = 3 * i // 2
        norm[r : r + 2, :] = norm[r : r + 2, :] + far[i, 0:2, :]
    norm_out[...] = norm[0:24, :].astype(jnp.bfloat16)

    for g in (0, 1):
        for u, (_, _, s, _) in enumerate(UNITS):
            arrived(g, u, F, at(s, 1, 0))
        give(g, 1, 1)
        give(g, 3, 1)
        take()
        take()
    for g in (0, 1):
        for u in range(len(UNITS)):
            arrived(g, u, G, at(2, 1, 0))
        give(g, 2, 1)
        take()
    while given:
        take()

    for g in (0, 1):
        pltpu.make_async_copy(part.at[g, pl.ds(0, 15)], part.at[g, pl.ds(0, 15)], part_send.at[g]).wait()
    pltpu.make_async_copy(near.at[pl.ds(0, 7)], near.at[pl.ds(0, 7)], norm_send.at[0]).wait()
    pltpu.make_async_copy(far.at[pl.ds(0, 15)], far.at[pl.ds(0, 15)], norm_send.at[1]).wait()
    for wait in late:
        wait()


def keep(*refs):
    n = len(refs) // 2
    copies = [pltpu.make_async_copy(refs[i], refs[n + i], refs[-1].at[i]) for i in range(n)]
    for cp in copies:
        cp.start()
    for cp in copies:
        cp.wait()


def per_device(d_model, *args):
    rows, cols = args[0].shape
    f32, bf16 = jnp.float32, jnp.bfloat16
    any_space, vmem = pl.BlockSpec(memory_space=pl.ANY), pl.BlockSpec(memory_space=pltpu.VMEM)
    dma = pltpu.SemaphoreType.DMA
    shapes = (
        ((16, rows, cols), bf16),
        ((16, rows, cols), bf16),
        ((1, cols), f32),
        ((1, cols), f32),
        ((24, 128), bf16),
        ((rows, cols), f32),
        ((rows, cols), f32),
    )
    args = (*args[:6], *(a.reshape(1, -1) for a in args[6:]))
    args = [pltpu.with_memory_space_constraint(a, pltpu.HBM) for a in args]
    held = pl.pallas_call(
        functools.partial(kernel, d_model),
        name="step",
        out_shape=tuple(pltpu.VMEM(*shape) for shape in shapes),
        in_specs=[any_space] * 8,
        out_specs=[vmem] * 7,
        scratch_shapes=[
            *[pltpu.VMEM((rows, cols), f32)] * 4,
            *[pltpu.VMEM((1, 24), f32)] * 2,
            pltpu.VMEM((2, 16, 1, cols), f32),
            pltpu.VMEM((8, 128), f32),
            pltpu.VMEM((8, 8, 128), f32),
            pltpu.VMEM((16, 8, 128), f32),
            pltpu.VMEM((32, 128), f32),
            dma((8,)), dma((2, 4, 7)), dma((2, 4, 7)), dma((2,)), dma((2,)), dma((2,)), dma((2,)), dma((2, 8)), dma((2, 8)),
        ],
        compiler_params=pltpu.CompilerParams(collective_id=0, has_side_effects=True, vmem_limit_bytes=16 * 2**20),
    )(*args)
    outs = pl.pallas_call(
        keep,
        name="keep",
        out_shape=tuple(jax.ShapeDtypeStruct(*shape) for shape in shapes),
        in_specs=[vmem] * 7,
        out_specs=[any_space] * 7,
        scratch_shapes=[dma((7,))],
        compiler_params=pltpu.CompilerParams(has_side_effects=True, vmem_limit_bytes=2**20),
    )(*[pltpu.with_memory_space_constraint(a, pltpu.VMEM) for a in held])
    serving_gate, serving_up, scale_gate, scale_up, norm, whole_gate, whole_up = outs
    return (
        serving_gate.reshape(16 * rows, cols),
        serving_up.reshape(16 * rows, cols),
        scale_gate.reshape(cols),
        scale_up.reshape(cols),
        norm.reshape(-1),
        whole_gate,
        whole_up,
    )


def solution(mesh):
    split = P("fsdp", "tp")
    return jax.shard_map(
        functools.partial(per_device, 3072),
        mesh=mesh,
        in_specs=(split,) * 6 + (P(("fsdp", "tp")),) * 2,
        out_specs=(P(None, "tp"), P(None, "tp"), P("tp"), P("tp"), P(), split, split),
        check_vma=False,
    )
```

time: 145 us -> 66.2 us (0.46)
  blocking collectives: 116 us -> 0 us
  Pallas kernels: 0 us -> 65.4 us
  between operations: 14.2 us -> 0.64 us
  local copies, waits for them, and re-layouts: 10.8 us -> 0 us
  other arithmetic: 4.05 us -> 0 us
    unnamed x1 -> x0, blocking collectives: 99.9 us -> none
    pallas_call x0 -> x2, Pallas kernels: none -> 65.4 us  [the longest x1 60.3 us: per_device(): pl.pallas_call(functools.partial(kernel, d_model), name='step', out_shape...]
    all_to_all x1 -> x0, blocking collectives: 15.8 us -> none  [from_everyone(): lax.all_to_all(jnp.broadcast_to(shard[None], (length, *shard.shape)), axi...]
    split x1 -> x0, local copies, waits for them, and re-layouts: 10.4 us -> none  [sent_together(): jnp.split(lax.all_gather(both, axis, axis=dim, tiled=True), ends, axis=al...]
    reduce_sum x2 -> x0, other arithmetic: 2.96 us -> none  [the longest x1 2.87 us: per_device(): jnp.sum(jnp.abs(whole_up), axis=0)]
  transfers between devices with their start and end apart: 1 -> 0, of which waited for: 0 -> 0; matrix products, arithmetic and copies ran while one was open for 0% -> 0% of each run, Pallas kernels for 0% -> 0%
where the time goes in v1:
time: 66.2 us; the launch traced here: 66.1 us
  Pallas kernels  65.4 us (99%)
    pallas_call x1, Pallas kernels, per_device(): pl.pallas_call(functools.partial(kernel, d_model), name='step', out_shape...  60.3 us
    pallas_call x1, Pallas kernels, per_device(): pl.pallas_call(keep, name='keep', out_shape=tuple((jax.ShapeDtypeStruct(*...  5.16 us

profile of v1, /device:TPU:1, one launch (start us, length us, event | category | flops | bytes accessed | tf_op | source)
XLA Modules:
  0.0 66.1 jit_solution(4688546549375526502)
XLA Ops:
  0.6 60.3 %step.1 = (bf16[16,192,1024]{2,1,0:T(8,128)(2,1)S(1)}, bf16[16,192,1024]{2,1,0:T(8,128)(2,1)S(1)}, f32[1,1024]{1,0:T(1,128)S(1)}, f32[1,1024]{1,0:T(1,128)S(1)},...) custom-call(f32[192,1024]{1,0:T(8,128)} %wg.1, f32[192,1024]{1,0:T(8,128)} %fg.1, ...), custom_call_target="tpu_custom_call" | custom-call | tf_op jit(solution)/shard_map/step/pallas_call | solution.py:221
  60.9 5.2 %keep.1 = (bf16[16,192,1024]{2,1,0:T(8,128)(2,1)}, bf16[16,192,1024]{2,1,0:T(8,128)(2,1)}, f32[1,1024]{1,0:T(1,128)}, f32[1,1024]{1,0:T(1,128)}, bf16[24,128]{1,...) custom-call(bf16[16,192,1024]{2,1,0:T(8,128)(2,1)S(1)} %get-tuple-element.21.refs_0_, ...), custom_call_target="tpu_custom_call" | custom-call | tf_op jit(solution)/shard_map/keep/pallas_call | solution.py:239

commit v2 on v1

v2 whole, which is shorter than its diff:
```python
import functools

import jax
import jax.numpy as jnp
from jax import lax
from jax.experimental import pallas as pl
from jax.experimental.pallas import tpu as pltpu
from jax.sharding import PartitionSpec as P

MESH = pl.DeviceIdType.MESH
LEARN_RATE = 0.25
HOLD_RATE = 0.9

UNITS = ((0, 64, 1, False), (96, 64, -1, False), (64, 32, 1, True), (160, 32, -1, True))
KINDS = "ABCDEFG"


def semaphore_of(kind, u):
    three = UNITS[u][3]
    k = KINDS.index(kind)
    if kind in "AE" or (kind == "B" and three) or (kind == "C" and not three):
        return (k, u)
    return (k, "late" if kind in "FG" and three else "all")


SEMAPHORES = sorted({semaphore_of(kind, u) for kind in KINDS for u in range(4)}, key=str)
TOGETHER = {key: tuple((KINDS[key[0]], u) for u in range(4) if semaphore_of(KINDS[key[0]], u) == key) for key in SEMAPHORES}


def kernel(
    d_model, wg, fg, sg, wu, fu, su, nt, ns,
    serve_g, serve_u, scale_g, scale_u, norm_out, whole_g, whole_u,
    a1, a2, b1, b2, n0, n1, part, own_norm, near, far, norm,
    in_sem, sent, tree_recv, part_recv, norm_send, norm_recv, d2d_recv, here,
):
    f, t = lax.axis_index("fsdp"), lax.axis_index("tp")
    y, p, c = f // 4, (f // 2) % 2, f % 2

    def at(dy, dp, dc):
        return ((y + dy + 4) % 4) * 4 + ((p + dp) % 2) * 2 + (c + dc) % 2

    peers = [at(dy, dp, dc) for dy in (2, 1, 3, 0) for dp in (1, 0) for dc in (1, 0) if (dy, dp, dc) != (0, 0, 0)]

    barrier = pltpu.get_barrier_semaphore()
    for q in peers:
        pl.semaphore_signal(barrier, inc=1, device_id=(q, t), device_id_type=MESH)
    for q in range(1, 8):

        @pl.when(t < q)
        def _(q=q):
            pl.semaphore_signal(barrier, inc=1, device_id=(f, q), device_id_type=MESH)

    serve, scale = (serve_g, serve_u), (scale_g, scale_u)
    pairs = ((wg, whole_g), (fg, a1), (sg, a2), (wu, whole_u), (fu, b1), (su, b2), (nt, n0), (ns, n1))
    loads = [pltpu.make_async_copy(src, dst, in_sem.at[i]) for i, (src, dst) in enumerate(pairs)]
    for load in loads:
        load.start()

    def remote(src, dst, send, recv, q):
        return pltpu.make_async_remote_copy(
            src_ref=src, dst_ref=dst, send_sem=send, recv_sem=recv, device_id=(q, t), device_id_type=MESH
        )

    def update(w, m1, m2, g):
        whole = w[...] - LEARN_RATE * (HOLD_RATE * m1[...] + m2[...])
        w[...] = whole
        part[g, f] = jnp.sum(jnp.abs(whole), axis=0, keepdims=True)

    def share(g):
        for q in peers:
            remote(part.at[g, f], part.at[g, f], sent.at[2], part_recv.at[g], q).start()

    def narrow(g, w):
        pltpu.make_async_copy(part.at[g, pl.ds(0, 15)], part.at[g, pl.ds(0, 15)], part_recv.at[g]).wait()
        mean = jnp.sum(part[g], axis=0) / d_model
        scale[g][...] = mean
        serve[g][f] = (w[...] * (1.0 / mean)).astype(jnp.bfloat16)

    def rows(g, u, block):
        return serve[g].at[block, pl.ds(UNITS[u][0], UNITS[u][1])]

    def send(g, u, kind, block, q):
        k = SEMAPHORES.index(semaphore_of(kind, u))
        remote(rows(g, u, block), rows(g, u, block), sent.at[g], tree_recv.at[g, k], q).start()

    def arrived(g, kind, u):
        key = semaphore_of(kind, u)
        total = sum(UNITS[v][1] for _, v in TOGETHER[key])
        ref = serve[g].at[0, pl.ds(0, total)]
        pltpu.make_async_copy(ref, ref, tree_recv.at[g, SEMAPHORES.index(key)]).wait()

    def give(g, dy, dp, units=None):
        block, k = at(dy, dp, 0), dy * 2 + dp
        for ref in [serve[g].at[block]] if units is None else [rows(g, u, block) for u in units]:
            remote(ref, ref, sent.at[g], d2d_recv.at[g, k], at(0, 0, 1)).start()

    def own(g):
        for u, (_, _, s, _) in enumerate(UNITS):
            send(g, u, "A", f, at(s, 0, 0))
            send(g, u, "C", f, at(0, 1, 0))
            send(g, u, "B", f, at(-s, 0, 0))

    for load in loads[:3]:
        load.wait()
    update(whole_g, a1, a2, 0)
    pl.semaphore_wait(barrier, len(peers) + t)
    share(0)
    for load in loads[3:6]:
        load.wait()
    update(whole_u, b1, b2, 1)
    share(1)
    for q in range(7):

        @pl.when(t > q)
        def _(q=q):
            pl.semaphore_signal(here, inc=1, device_id=(f, q), device_id_type=MESH)

    for load in loads[6:]:
        load.wait()
    own_norm[...] = jnp.zeros_like(own_norm)
    own_norm[0:1, 0:24] = (n0[...] + n1[...]).astype(jnp.bfloat16).astype(jnp.float32)
    first = 24 * t + 64 * (f % 2)
    rolled = pltpu.roll(jnp.broadcast_to(own_norm[0:1, :], (8, 128)), first % 128, 1)
    place = 128 * lax.broadcasted_iota(jnp.int32, (8, 128), 0) + lax.broadcasted_iota(jnp.int32, (8, 128), 1) - first
    near[t] = jnp.where((place >= 0) & (place < 24), rolled, 0.0)[0:2]

    narrow(0, whole_g)
    own(0)
    narrow(1, whole_u)
    own(1)
    for g in (0, 1):
        give(g, 0, 0)

    @pl.when(t < 7)
    def _():
        pl.semaphore_wait(here, 7 - t)

    for k in range(1, 8):
        pltpu.make_async_remote_copy(
            src_ref=near.at[t], dst_ref=near.at[t], send_sem=norm_send.at[0], recv_sem=norm_recv.at[0],
            device_id=(f, (t + k) % 8), device_id_type=MESH,
        ).start()

    for g in (0, 1):
        for u, (_, _, s, three) in enumerate(UNITS):
            arrived(g, "A", u)
            send(g, u, "D", at(-s, 0, 0), at(s, 0, 0))
            send(g, u, "E", at(-s, 0, 0), at(0, 1, 0))
            if not three:
                arrived(g, "C", u)
                send(g, u, "F", at(0, 1, 0), at(-s, 0, 0))
        arrived(g, "C", 2)
        give(g, 0, 1)
    for g in (0, 1):
        for u in (2, 3):
            s = UNITS[u][2]
            arrived(g, "B", u)
            send(g, u, "F", at(s, 0, 0), at(0, 1, 0))
        arrived(g, "B", 0)
        give(g, 1, 0)
        give(g, 3, 0)

    pltpu.make_async_copy(near.at[pl.ds(0, 7)], near.at[pl.ds(0, 7)], norm_recv.at[0]).wait()
    far[f] = jnp.sum(near[...], axis=0)
    for q in peers:
        remote(far.at[f], far.at[f], norm_send.at[1], norm_recv.at[1], q).start()

    for g in (0, 1):
        for u, (_, _, s, _) in enumerate(UNITS):
            arrived(g, "E", u)
            send(g, u, "G", at(-s, 1, 0), at(s, 0, 0))
    for g in (0, 1):
        arrived(g, "D", 0)
        give(g, 2, 0)

    pltpu.make_async_copy(far.at[pl.ds(0, 15)], far.at[pl.ds(0, 15)], norm_recv.at[1]).wait()
    norm[...] = jnp.zeros_like(norm)
    for i in range(16):
        r = 3 * i // 2
        norm[r : r + 2, :] = norm[r : r + 2, :] + far[i]
    norm_out[...] = norm[0:24, :].astype(jnp.bfloat16)

    for g in (0, 1):
        arrived(g, "F", 0)
        give(g, 1, 1, (0, 1, 3))
        give(g, 3, 1, (0, 1, 2))
    for g in (0, 1):
        arrived(g, "G", 0)
        give(g, 2, 1, (0, 1))
        arrived(g, "F", 2)
        give(g, 1, 1, (2,))
        give(g, 3, 1, (3,))
        arrived(g, "G", 2)
        give(g, 2, 1, (2, 3))

    for g in (0, 1):
        for k in range(8):
            pltpu.make_async_copy(serve[g].at[0], serve[g].at[0], d2d_recv.at[g, k]).wait()
    for g in (0, 1):
        pltpu.make_async_copy(serve[g].at[pl.ds(0, 15)], serve[g].at[pl.ds(0, 15)], sent.at[g]).wait()
    pltpu.make_async_copy(part.at[:, pl.ds(0, 15)], part.at[:, pl.ds(0, 15)], sent.at[2]).wait()
    pltpu.make_async_copy(near.at[pl.ds(0, 7)], near.at[pl.ds(0, 7)], norm_send.at[0]).wait()
    pltpu.make_async_copy(far.at[pl.ds(0, 15)], far.at[pl.ds(0, 15)], norm_send.at[1]).wait()


def keep(*refs):
    n = len(refs) // 2
    copies = [pltpu.make_async_copy(refs[i], refs[n + i], refs[-1].at[i]) for i in range(n)]
    for cp in copies:
        cp.start()
    for cp in copies:
        cp.wait()


def per_device(d_model, *args):
    rows, cols = args[0].shape
    f32, bf16 = jnp.float32, jnp.bfloat16
    any_space, vmem = pl.BlockSpec(memory_space=pl.ANY), pl.BlockSpec(memory_space=pltpu.VMEM)
    dma = pltpu.SemaphoreType.DMA
    shapes = (
        ((16, rows, cols), bf16),
        ((16, rows, cols), bf16),
        ((1, cols), f32),
        ((1, cols), f32),
        ((24, 128), bf16),
        ((rows, cols), f32),
        ((rows, cols), f32),
    )
    args = (*args[:6], *(a.reshape(1, -1) for a in args[6:]))
    args = [pltpu.with_memory_space_constraint(a, pltpu.HBM) for a in args]
    held = pl.pallas_call(
        functools.partial(kernel, d_model),
        name="step",
        out_shape=tuple(pltpu.VMEM(*shape) for shape in shapes),
        in_specs=[any_space] * 8,
        out_specs=[vmem] * 7,
        scratch_shapes=[
            *[pltpu.VMEM((rows, cols), f32)] * 4,
            *[pltpu.VMEM((1, 24), f32)] * 2,
            pltpu.VMEM((2, 16, 1, cols), f32),
            pltpu.VMEM((8, 128), f32),
            pltpu.VMEM((8, 2, 128), f32),
            pltpu.VMEM((16, 2, 128), f32),
            pltpu.VMEM((32, 128), f32),
            dma((8,)), dma((3,)), dma((2, len(SEMAPHORES))), dma((2,)), dma((2,)), dma((2,)), dma((2, 8)), pltpu.SemaphoreType.REGULAR,
        ],
        compiler_params=pltpu.CompilerParams(collective_id=0, has_side_effects=True, vmem_limit_bytes=16 * 2**20),
    )(*args)
    outs = pl.pallas_call(
        keep,
        name="keep",
        out_shape=tuple(jax.ShapeDtypeStruct(*shape) for shape in shapes),
        in_specs=[vmem] * 7,
        out_specs=[any_space] * 7,
        scratch_shapes=[dma((7,))],
        compiler_params=pltpu.CompilerParams(has_side_effects=True, vmem_limit_bytes=2**20),
    )(*[pltpu.with_memory_space_constraint(a, pltpu.VMEM) for a in held])
    serving_gate, serving_up, scale_gate, scale_up, norm, whole_gate, whole_up = outs
    return (
        serving_gate.reshape(16 * rows, cols),
        serving_up.reshape(16 * rows, cols),
        scale_gate.reshape(cols),
        scale_up.reshape(cols),
        norm.reshape(-1),
        whole_gate,
        whole_up,
    )


def solution(mesh):
    split = P("fsdp", "tp")
    return jax.shard_map(
        functools.partial(per_device, 3072),
        mesh=mesh,
        in_specs=(split,) * 6 + (P(("fsdp", "tp")),) * 2,
        out_specs=(P(None, "tp"), P(None, "tp"), P("tp"), P("tp"), P(), split, split),
        check_vma=False,
    )
```

time: 66.2 us -> 66 us (level)
  no operation moved by 1% of the time
where the time goes in v2:
time: 66 us; the launch traced here: 65.9 us
  Pallas kernels  65.2 us (99%)
    pallas_call x1, Pallas kernels, per_device(): pl.pallas_call(functools.partial(kernel, d_model), name='step', out_shape...  60.1 us
    pallas_call x1, Pallas kernels, per_device(): pl.pallas_call(keep, name='keep', out_shape=tuple((jax.ShapeDtypeStruct(*...  5.16 us

profile of v2, /device:TPU:1, one launch (start us, length us, event | category | flops | bytes accessed | tf_op | source)
XLA Modules:
  0.0 65.9 jit_solution(2752147683073420496)
XLA Ops:
  0.6 60.1 %step.1 = (bf16[16,192,1024]{2,1,0:T(8,128)(2,1)S(1)}, bf16[16,192,1024]{2,1,0:T(8,128)(2,1)S(1)}, f32[1,1024]{1,0:T(1,128)S(1)}, f32[1,1024]{1,0:T(1,128)S(1)},...) custom-call(f32[192,1024]{1,0:T(8,128)} %wg.1, f32[192,1024]{1,0:T(8,128)} %fg.1, ...), custom_call_target="tpu_custom_call" | custom-call | tf_op jit(solution)/shard_map/step/pallas_call | solution.py:231
  60.7 5.2 %keep.1 = (bf16[16,192,1024]{2,1,0:T(8,128)(2,1)}, bf16[16,192,1024]{2,1,0:T(8,128)(2,1)}, f32[1,1024]{1,0:T(1,128)}, f32[1,1024]{1,0:T(1,128)}, bf16[24,128]{1,...) custom-call(bf16[16,192,1024]{2,1,0:T(8,128)(2,1)S(1)} %get-tuple-element.21.refs_0_, ...), custom_call_target="tpu_custom_call" | custom-call | tf_op jit(solution)/shard_map/keep/pallas_call | solution.py:249

commit v3 on v2

--- a/solution.py
+++ b/solution.py
@@ -11,12 +11,15 @@
 LEARN_RATE = 0.25
 HOLD_RATE = 0.9
 
-UNITS = ((0, 64, 1, False), (96, 64, -1, False), (64, 32, 1, True), (160, 32, -1, True))
+UNITS = (
+    ((0, 72, 1, False), (96, 72, -1, False), (72, 24, 1, True), (168, 24, -1, True)),
+    ((0, 64, 1, False), (96, 64, -1, False), (64, 32, 1, True), (160, 32, -1, True)),
+)
 KINDS = "ABCDEFG"
 
 
 def semaphore_of(kind, u):
-    three = UNITS[u][3]
+    three = UNITS[0][u][3]
     k = KINDS.index(kind)
     if kind in "AE" or (kind == "B" and three) or (kind == "C" and not three):
         return (k, u)
@@ -77,7 +80,7 @@
         serve[g][f] = (w[...] * (1.0 / mean)).astype(jnp.bfloat16)
 
     def rows(g, u, block):
-        return serve[g].at[block, pl.ds(UNITS[u][0], UNITS[u][1])]
+        return serve[g].at[block, pl.ds(UNITS[g][u][0], UNITS[g][u][1])]
 
     def send(g, u, kind, block, q):
         k = SEMAPHORES.index(semaphore_of(kind, u))
@@ -85,7 +88,7 @@
 
     def arrived(g, kind, u):
         key = semaphore_of(kind, u)
-        total = sum(UNITS[v][1] for _, v in TOGETHER[key])
+        total = sum(UNITS[g][v][1] for _, v in TOGETHER[key])
         ref = serve[g].at[0, pl.ds(0, total)]
         pltpu.make_async_copy(ref, ref, tree_recv.at[g, SEMAPHORES.index(key)]).wait()
 
@@ -95,7 +98,7 @@
             remote(ref, ref, sent.at[g], d2d_recv.at[g, k], at(0, 0, 1)).start()
 
     def own(g):
-        for u, (_, _, s, _) in enumerate(UNITS):
+        for u, (_, _, s, _) in enumerate(UNITS[g]):
             send(g, u, "A", f, at(s, 0, 0))
             send(g, u, "C", f, at(0, 1, 0))
             send(g, u, "B", f, at(-s, 0, 0))
@@ -126,11 +129,6 @@
 
     narrow(0, whole_g)
     own(0)
-    narrow(1, whole_u)
-    own(1)
-    for g in (0, 1):
-        give(g, 0, 0)
-
     @pl.when(t < 7)
     def _():
         pl.semaphore_wait(here, 7 - t)
@@ -140,9 +138,13 @@
             src_ref=near.at[t], dst_ref=near.at[t], send_sem=norm_send.at[0], recv_sem=norm_recv.at[0],
             device_id=(f, (t + k) % 8), device_id_type=MESH,
         ).start()
-
-    for g in (0, 1):
-        for u, (_, _, s, three) in enumerate(UNITS):
+    narrow(1, whole_u)
+    own(1)
+    for g in (0, 1):
+        give(g, 0, 0)
+
+    for g in (0, 1):
+        for u, (_, _, s, three) in enumerate(UNITS[g]):
             arrived(g, "A", u)
             send(g, u, "D", at(-s, 0, 0), at(s, 0, 0))
             send(g, u, "E", at(-s, 0, 0), at(0, 1, 0))
@@ -151,22 +153,22 @@
                 send(g, u, "F", at(0, 1, 0), at(-s, 0, 0))
         arrived(g, "C", 2)
         give(g, 0, 1)
+        if g == 0:
+            pltpu.make_async_copy(near.at[pl.ds(0, 7)], near.at[pl.ds(0, 7)], norm_recv.at[0]).wait()
+            far[f] = jnp.sum(near[...], axis=0)
+            for q in peers:
+                remote(far.at[f], far.at[f], norm_send.at[1], norm_recv.at[1], q).start()
     for g in (0, 1):
         for u in (2, 3):
-            s = UNITS[u][2]
+            s = UNITS[g][u][2]
             arrived(g, "B", u)
             send(g, u, "F", at(s, 0, 0), at(0, 1, 0))
         arrived(g, "B", 0)
         give(g, 1, 0)
         give(g, 3, 0)
 
-    pltpu.make_async_copy(near.at[pl.ds(0, 7)], near.at[pl.ds(0, 7)], norm_recv.at[0]).wait()
-    far[f] = jnp.sum(near[...], axis=0)
-    for q in peers:
-        remote(far.at[f], far.at[f], norm_send.at[1], norm_recv.at[1], q).start()
-
-    for g in (0, 1):
-        for u, (_, _, s, _) in enumerate(UNITS):
+    for g in (0, 1):
+        for u, (_, _, s, _) in enumerate(UNITS[g]):
             arrived(g, "E", u)
             send(g, u, "G", at(-s, 1, 0), at(s, 0, 0))
     for g in (0, 1):

time: 66 us -> 60.7 us (0.920)
  Pallas kernels: 65.2 us -> 60 us
    pallas_call x1, Pallas kernels: 60.1 us -> 54.8 us  [per_device(): pl.pallas_call(functools.partial(kernel, d_model), name='step', out_shape...]
where the time goes in v3:
time: 60.7 us; the launch traced here: 60.6 us
  Pallas kernels  60 us (99%)
  between operations  0.64 us (1%)
    pallas_call x1, Pallas kernels, per_device(): pl.pallas_call(functools.partial(kernel, d_model), name='step', out_shape...  54.8 us
    pallas_call x1, Pallas kernels, per_device(): pl.pallas_call(keep, name='keep', out_shape=tuple((jax.ShapeDtypeStruct(*...  5.16 us

profile of v3, /device:TPU:1, one launch (start us, length us, event | category | flops | bytes accessed | tf_op | source)
XLA Modules:
  0.0 60.6 jit_solution(11928281880981267987)
XLA Ops:
  0.6 54.8 %step.1 = (bf16[16,192,1024]{2,1,0:T(8,128)(2,1)S(1)}, bf16[16,192,1024]{2,1,0:T(8,128)(2,1)S(1)}, f32[1,1024]{1,0:T(1,128)S(1)}, f32[1,1024]{1,0:T(1,128)S(1)},...) custom-call(f32[192,1024]{1,0:T(8,128)} %wg.1, f32[192,1024]{1,0:T(8,128)} %fg.1, ...), custom_call_target="tpu_custom_call" | custom-call | tf_op jit(solution)/shard_map/step/pallas_call | solution.py:233
  55.4 5.2 %keep.1 = (bf16[16,192,1024]{2,1,0:T(8,128)(2,1)}, bf16[16,192,1024]{2,1,0:T(8,128)(2,1)}, f32[1,1024]{1,0:T(1,128)}, f32[1,1024]{1,0:T(1,128)}, bf16[24,128]{1,...) custom-call(bf16[16,192,1024]{2,1,0:T(8,128)(2,1)S(1)} %get-tuple-element.21.refs_0_, ...), custom_call_target="tpu_custom_call" | custom-call | tf_op jit(solution)/shard_map/keep/pallas_call | solution.py:251

commit v4 on v3

v4 whole, which is shorter than its diff:
```python
import functools

import jax
import jax.numpy as jnp
from jax import lax
from jax.experimental import pallas as pl
from jax.experimental.pallas import tpu as pltpu
from jax.sharding import PartitionSpec as P

MESH = pl.DeviceIdType.MESH
LEARN_RATE = 0.25
HOLD_RATE = 0.9

UNITS = (
    ((0, 48, 1, 2), (96, 56, -1, 2), (72, 24, 1, 3), (168, 24, -1, 3), (48, 24, 1, 2), (152, 16, -1, 2)),
    ((0, 64, 1, 2), (96, 64, -1, 2), (64, 32, 1, 3), (160, 32, -1, 3)),
)
EARLY = (4, 5)
EARLY_AT = (0, 24)
EARLY_ROWS = 40
KINDS = "ABCDEFG"


def semaphore_of(g, kind, u):
    three = UNITS[g][u][3] == 3
    if kind in "AE" or (kind == "B" and three) or (kind == "C" and not three):
        return kind, u
    return kind, 9 if kind in "FG" and three else 8


SEMAPHORES, TOGETHER = [], []
for matrix in (0, 1):
    rows_of = {}
    for kind in KINDS:
        for u, unit in enumerate(UNITS[matrix]):
            if matrix == 1 or u not in EARLY or kind not in "ABC":
                key = semaphore_of(matrix, kind, u)
                rows_of[key] = rows_of.get(key, 0) + unit[1]
    SEMAPHORES.append(sorted(rows_of))
    TOGETHER.append(rows_of)


def kernel(
    d_model, wg, fg, sg, wu, fu, su, nt, ns,
    serve_g, serve_u, scale_g, scale_u, norm_out, whole_g, whole_u,
    a1, a2, b1, b2, n0, n1, direct, part, total, own_norm, near, far, image, stack, norm, early,
    in_sem, sent, tree_recv, sums_recv, norm_sent, norm_recv, d2d_recv, early_recv, here,
):
    f, t = lax.axis_index("fsdp"), lax.axis_index("tp")
    y, p, c = f // 4, (f // 2) % 2, f % 2

    def at(dy, dp, dc):
        return ((y + dy + 4) % 4) * 4 + ((p + dp) % 2) * 2 + (c + dc) % 2

    peers = [at(dy, dp, dc) for dy in (2, 1, 3, 0) for dp in (1, 0) for dc in (1, 0) if (dy, dp, dc) != (0, 0, 0)]
    row, row_peers = f % 4, [at(0, 1, 1), at(0, 1, 0), at(0, 0, 1)]
    ring_peers = [at(2, 0, 0), at(1, 0, 0), at(3, 0, 0)]
    z, side = t // 2, t % 2
    tp_peers = [(t + 2 * k) % 8 for k in range(1, 4)] + [2 * z + 1 - side]

    barrier = pltpu.get_barrier_semaphore()
    for q in peers:
        pl.semaphore_signal(barrier, inc=1, device_id=(q, t), device_id_type=MESH)
    for q in tp_peers:

        @pl.when(t < q)
        def _(q=q):
            pl.semaphore_signal(barrier, inc=1, device_id=(f, q), device_id_type=MESH)

    serve, scale = (serve_g, serve_u), (scale_g, scale_u)
    pairs = ((wg, whole_g), (fg, a1), (sg, a2), (wu, whole_u), (fu, b1), (su, b2), (nt, n0), (ns, n1))
    loads = [pltpu.make_async_copy(src, dst, in_sem.at[i]) for i, (src, dst) in enumerate(pairs)]
    for load in loads:
        load.start()

    def remote(src, dst, send, recv, q):
        return pltpu.make_async_remote_copy(
            src_ref=src, dst_ref=dst, send_sem=send, recv_sem=recv, device_id=(q, t), device_id_type=MESH
        )

    def update(w, m1, m2, g):
        whole = w[...] - LEARN_RATE * (HOLD_RATE * m1[...] + m2[...])
        w[...] = whole
        sums = jnp.sum(jnp.abs(whole), axis=0, keepdims=True)
        if g == 0:
            direct[f] = sums
        else:
            part[row] = sums

    def share(slots, slot, recv, to, send=None):
        for q in to:
            remote(slots.at[slot], slots.at[slot], sent.at[2] if send is None else send, recv, q).start()

    def wait_slots(slots, n, sem):
        pltpu.make_async_copy(slots.at[pl.ds(0, n)], slots.at[pl.ds(0, n)], sem).wait()

    def leave_early(i):
        r, n, s, _ = UNITS[0][EARLY[i]]
        for k, q in enumerate((at(s, 0, 0), at(-s, 0, 0), at(0, 1, 0))):
            remote(whole_g.at[pl.ds(r, n)], early.at[k, pl.ds(EARLY_AT[i], n)], sent.at[3], early_recv.at[0], q).start()

    def narrow(g, w):
        slots, n = (direct, 15) if g == 0 else (total, 3)
        wait_slots(slots, n, sums_recv.at[g])
        mean = jnp.sum(slots[...], axis=0) / d_model
        scale[g][...] = mean
        inverse = 1.0 / mean
        serve[g][f] = (w[...] * inverse).astype(jnp.bfloat16)
        return inverse

    def rows(g, u, block):
        return serve[g].at[block, pl.ds(UNITS[g][u][0], UNITS[g][u][1])]

    def send(g, u, kind, block, q):
        k = SEMAPHORES[g].index(semaphore_of(g, kind, u))
        remote(rows(g, u, block), rows(g, u, block), sent.at[g], tree_recv.at[g, k], q).start()

    def arrived(g, kind, u):
        key = semaphore_of(g, kind, u)
        ref = serve[g].at[0, pl.ds(0, TOGETHER[g][key])]
        pltpu.make_async_copy(ref, ref, tree_recv.at[g, SEMAPHORES[g].index(key)]).wait()

    def give(g, dy, dp, units=None):
        block = at(dy, dp, 0)
        for ref in [serve[g].at[block]] if units is None else [rows(g, u, block) for u in units]:
            remote(ref, ref, sent.at[g], d2d_recv.at[g], at(0, 0, 1)).start()

    def own(g):
        for u, (_, _, s, _) in enumerate(UNITS[g][:4]):
            send(g, u, "A", f, at(s, 0, 0))
            send(g, u, "C", f, at(0, 1, 0))
            send(g, u, "B", f, at(-s, 0, 0))

    for load in loads[:3]:
        load.wait()
    update(whole_g, a1, a2, 0)
    pl.semaphore_wait(barrier, len(peers) + z + side)
    share(direct, f, sums_recv.at[0], peers)
    for load in loads[3:]:
        load.wait()
    update(whole_u, b1, b2, 1)
    share(part, row, sums_recv.at[2], row_peers)

    own_norm[...] = jnp.zeros_like(own_norm)
    own_norm[0:1, 0:24] = (n0[...] + n1[...]).astype(jnp.bfloat16).astype(jnp.float32)
    first = 24 * t + 64 * (f % 2)
    rolled = pltpu.roll(jnp.broadcast_to(own_norm[0:1, :], (8, 128)), first % 128, 1)
    place = 128 * lax.broadcasted_iota(jnp.int32, (8, 128), 0) + lax.broadcasted_iota(jnp.int32, (8, 128), 1) - first
    near[row] = jnp.where((place >= 0) & (place < 24), rolled, 0.0)[0:2]
    share(near, row, norm_recv.at[0], row_peers, norm_sent.at[0])
    leave_early(0)
    leave_early(1)
    for q in tp_peers:

        @pl.when(t > q)
        def _(q=q):
            pl.semaphore_signal(here, inc=1, device_id=(f, q), device_id_type=MESH)

    wait_slots(part, 3, sums_recv.at[2])
    total[y] = jnp.sum(part[...], axis=0)
    share(total, y, sums_recv.at[1], ring_peers)
    wait_slots(near, 3, norm_recv.at[0])
    far[y] = near[...]
    share(far, y, norm_recv.at[1], ring_peers, norm_sent.at[1])

    inverse = narrow(0, whole_g)
    own(0)
    pltpu.make_async_copy(early, early, early_recv.at[0]).wait()
    for i, u in enumerate(EARLY):
        r, n, s, _ = UNITS[0][u]
        for k, q in enumerate((at(-s, 0, 0), at(s, 0, 0), at(0, 1, 0))):
            serve_g[q, r : r + n] = (early[k, EARLY_AT[i] : EARLY_AT[i] + n] * inverse).astype(jnp.bfloat16)
    for u in EARLY:
        s = UNITS[0][u][2]
        send(0, u, "D", at(-s, 0, 0), at(s, 0, 0))
        send(0, u, "E", at(-s, 0, 0), at(0, 1, 0))
        send(0, u, "F", at(0, 1, 0), at(-s, 0, 0))
    wait_slots(far, 3, norm_recv.at[1])
    norm[...] = jnp.zeros_like(norm)
    for i in range(16):
        r = 3 * i // 2
        norm[r : r + 2, :] = norm[r : r + 2, :] + far[i // 4, i % 4]
    image[0] = norm[0:24, :].astype(jnp.bfloat16)

    @pl.when(t < 7)
    def _():
        pl.semaphore_wait(here, 4 - z - side)

    def norm_to(src, dst, k, q):
        return pltpu.make_async_remote_copy(
            src_ref=src, dst_ref=dst, send_sem=norm_sent.at[k], recv_sem=norm_recv.at[k],
            device_id=(f, q), device_id_type=MESH,
        )

    norm_to(image.at[0], image.at[1], 2, tp_peers[3]).start()
    narrow(1, whole_u)
    own(1)
    for g in (0, 1):
        give(g, 0, 0)

    for g in (0, 1):
        for u, (_, _, s, crossings) in enumerate(UNITS[g][:4]):
            arrived(g, "A", u)
            send(g, u, "D", at(-s, 0, 0), at(s, 0, 0))
            send(g, u, "E", at(-s, 0, 0), at(0, 1, 0))
            if crossings == 2:
                arrived(g, "C", u)
                send(g, u, "F", at(0, 1, 0), at(-s, 0, 0))
        arrived(g, "C", 2)
        give(g, 0, 1)
    wait_slots(image, 1, norm_recv.at[2])
    stack[z] = (image[0].astype(jnp.float32) + image[1].astype(jnp.float32)).astype(jnp.bfloat16)
    for q in tp_peers[:3]:
        norm_to(stack.at[z], stack.at[z], 3, q).start()
    for g in (0, 1):
        for u in (2, 3):
            s = UNITS[g][u][2]
            arrived(g, "B", u)
            send(g, u, "F", at(s, 0, 0), at(0, 1, 0))
        arrived(g, "B", 0)
        give(g, 1, 0)
        give(g, 3, 0)

    for g in (0, 1):
        for u in (*EARLY, 0, 1, 2, 3) if g == 0 else range(4):
            s = UNITS[g][u][2]
            arrived(g, "E", u)
            send(g, u, "G", at(-s, 1, 0), at(s, 0, 0))
    for g in (0, 1):
        arrived(g, "D", 0)
        give(g, 2, 0)

    wait_slots(stack, 3, norm_recv.at[3])
    norm_out[...] = jnp.sum(stack[...].astype(jnp.float32), axis=0).astype(jnp.bfloat16)

    for g in (0, 1):
        arrived(g, "F", 0)
        both = (0, 1, *EARLY) if g == 0 else (0, 1)
        give(g, 1, 1, (*both, 3))
        give(g, 3, 1, (*both, 2))
    for g in (0, 1):
        arrived(g, "G", 0)
        give(g, 2, 1, (0, 1, *EARLY) if g == 0 else (0, 1))
        arrived(g, "F", 2)
        give(g, 1, 1, (2,))
        give(g, 3, 1, (3,))
        arrived(g, "G", 2)
        give(g, 2, 1, (2, 3))

    for g in (0, 1):
        pltpu.make_async_copy(serve[g].at[pl.ds(0, 8)], serve[g].at[pl.ds(0, 8)], d2d_recv.at[g]).wait()
    n = sum(unit[1] for unit in UNITS[0])
    blocks, rest = divmod(sum(TOGETHER[0].values()) + 8 * n, n)
    for ref, sem in (
        (serve_g.at[pl.ds(0, blocks)], sent.at[0]),
        (serve_g.at[0, pl.ds(0, rest)], sent.at[0]),
        (serve_u.at[pl.ds(0, 15)], sent.at[1]),
        (direct.at[pl.ds(0, 15)], sent.at[2]),
        (part.at[pl.ds(0, 3)], sent.at[2]),
        (total.at[pl.ds(0, 3)], sent.at[2]),
        (early, sent.at[3]),
        (near.at[pl.ds(0, 3)], norm_sent.at[0]),
        (far.at[pl.ds(0, 3)], norm_sent.at[1]),
        (image.at[0], norm_sent.at[2]),
        (stack.at[pl.ds(0, 3)], norm_sent.at[3]),
    ):
        pltpu.make_async_copy(ref, ref, sem).wait()


def keep(*refs):
    n = len(refs) // 2
    copies = [pltpu.make_async_copy(refs[i], refs[n + i], refs[-1].at[i]) for i in range(n)]
    for cp in copies:
        cp.start()
    for cp in copies:
        cp.wait()


def per_device(d_model, *args):
    rows, cols = args[0].shape
    f32, bf16 = jnp.float32, jnp.bfloat16
    any_space, vmem = pl.BlockSpec(memory_space=pl.ANY), pl.BlockSpec(memory_space=pltpu.VMEM)
    dma = pltpu.SemaphoreType.DMA
    shapes = (
        ((16, rows, cols), bf16),
        ((16, rows, cols), bf16),
        ((1, cols), f32),
        ((1, cols), f32),
        ((24, 128), bf16),
        ((rows, cols), f32),
        ((rows, cols), f32),
    )
    args = (*args[:6], *(a.reshape(1, -1) for a in args[6:]))
    args = [pltpu.with_memory_space_constraint(a, pltpu.HBM) for a in args]
    held = pl.pallas_call(
        functools.partial(kernel, d_model),
        name="step",
        out_shape=tuple(pltpu.VMEM(*shape) for shape in shapes),
        in_specs=[any_space] * 8,
        out_specs=[vmem] * 7,
        scratch_shapes=[
            *[pltpu.VMEM((rows, cols), f32)] * 4,
            *[pltpu.VMEM((1, 24), f32)] * 2,
            pltpu.VMEM((16, 1, cols), f32),
            pltpu.VMEM((4, 1, cols), f32),
            pltpu.VMEM((4, 1, cols), f32),
            pltpu.VMEM((8, 128), f32),
            pltpu.VMEM((4, 2, 128), f32),
            pltpu.VMEM((4, 4, 2, 128), f32),
            pltpu.VMEM((2, 24, 128), bf16),
            pltpu.VMEM((4, 24, 128), bf16),
            pltpu.VMEM((32, 128), f32),
            pltpu.VMEM((3, EARLY_ROWS, cols), f32),
            dma((8,)), dma((4,)), dma((2, max(map(len, SEMAPHORES)))), dma((3,)), dma((4,)), dma((4,)), dma((2,)), dma((1,)),
            pltpu.SemaphoreType.REGULAR,
        ],
        compiler_params=pltpu.CompilerParams(collective_id=0, has_side_effects=True, vmem_limit_bytes=16 * 2**20),
    )(*args)
    outs = pl.pallas_call(
        keep,
        name="keep",
        out_shape=tuple(jax.ShapeDtypeStruct(*shape) for shape in shapes),
        in_specs=[vmem] * 7,
        out_specs=[any_space] * 7,
        scratch_shapes=[dma((7,))],
        compiler_params=pltpu.CompilerParams(has_side_effects=True, vmem_limit_bytes=2**20),
    )(*[pltpu.with_memory_space_constraint(a, pltpu.VMEM) for a in held])
    serving_gate, serving_up, scale_gate, scale_up, norm, whole_gate, whole_up = outs
    return (
        serving_gate.reshape(16 * rows, cols),
        serving_up.reshape(16 * rows, cols),
        scale_gate.reshape(cols),
        scale_up.reshape(cols),
        norm.reshape(-1),
        whole_gate,
        whole_up,
    )


def solution(mesh):
    split = P("fsdp", "tp")
    return jax.shard_map(
        functools.partial(per_device, 3072),
        mesh=mesh,
        in_specs=(split,) * 6 + (P(("fsdp", "tp")),) * 2,
        out_specs=(P(None, "tp"), P(None, "tp"), P("tp"), P("tp"), P(), split, split),
        check_vma=False,
    )
```

time: 60.7 us -> 59.4 us (0.979)
  Pallas kernels: 60 us -> 58.6 us
    pallas_call x1, Pallas kernels: 54.8 us -> 53.5 us  [per_device(): pl.pallas_call(functools.partial(kernel, d_model), name='step', out_shape...]
where the time goes in v4:
time: 59.4 us; the launch traced here: 59.3 us
  Pallas kernels  58.6 us (99%)
  between operations  0.64 us (1%)
    pallas_call x1, Pallas kernels, per_device(): pl.pallas_call(functools.partial(kernel, d_model), name='step', out_shape...  53.5 us
    pallas_call x1, Pallas kernels, per_device(): pl.pallas_call(keep, name='keep', out_shape=tuple((jax.ShapeDtypeStruct(*...  5.16 us

profile of v4, /device:TPU:1, one launch (start us, length us, event | category | flops | bytes accessed | tf_op | source)
XLA Modules:
  0.0 59.3 jit_solution(6722390811902876489)
XLA Ops:
  0.6 53.5 %step.1 = (bf16[16,192,1024]{2,1,0:T(8,128)(2,1)S(1)}, bf16[16,192,1024]{2,1,0:T(8,128)(2,1)S(1)}, f32[1,1024]{1,0:T(1,128)S(1)}, f32[1,1024]{1,0:T(1,128)S(1)},...) custom-call(f32[192,1024]{1,0:T(8,128)} %wg.1, f32[192,1024]{1,0:T(8,128)} %fg.1, ...), custom_call_target="tpu_custom_call" | custom-call | tf_op jit(solution)/shard_map/step/pallas_call | solution.py:295
  54.1 5.2 %keep.1 = (bf16[16,192,1024]{2,1,0:T(8,128)(2,1)}, bf16[16,192,1024]{2,1,0:T(8,128)(2,1)}, f32[1,1024]{1,0:T(1,128)}, f32[1,1024]{1,0:T(1,128)}, bf16[24,128]{1,...) custom-call(bf16[16,192,1024]{2,1,0:T(8,128)(2,1)S(1)} %get-tuple-element.21.refs_0_, ...), custom_call_target="tpu_custom_call" | custom-call | tf_op jit(solution)/shard_map/keep/pallas_call | solution.py:319

commit v5 on v4

--- a/solution.py
+++ b/solution.py
@@ -12,20 +12,20 @@
 HOLD_RATE = 0.9
 
 UNITS = (
-    ((0, 48, 1, 2), (96, 56, -1, 2), (72, 24, 1, 3), (168, 24, -1, 3), (48, 24, 1, 2), (152, 16, -1, 2)),
+    ((0, 40, 1, 2), (96, 40, -1, 2), (64, 32, 1, 3), (160, 32, -1, 3), (40, 24, 1, 2), (136, 24, -1, 2)),
     ((0, 64, 1, 2), (96, 64, -1, 2), (64, 32, 1, 3), (160, 32, -1, 3)),
 )
 EARLY = (4, 5)
 EARLY_AT = (0, 24)
-EARLY_ROWS = 40
+EARLY_ROWS = 48
 KINDS = "ABCDEFG"
 
 
 def semaphore_of(g, kind, u):
     three = UNITS[g][u][3] == 3
-    if kind in "AE" or (kind == "B" and three) or (kind == "C" and not three):
-        return kind, u
-    return kind, 9 if kind in "FG" and three else 8
+    if kind in "AE" or (kind == "C" and not three):
+        return kind, u & 6 if u > 1 else u
+    return kind, 9 if kind in "BFG" and three else 8
 
 
 SEMAPHORES, TOGETHER = [], []
@@ -44,7 +44,7 @@
     d_model, wg, fg, sg, wu, fu, su, nt, ns,
     serve_g, serve_u, scale_g, scale_u, norm_out, whole_g, whole_u,
     a1, a2, b1, b2, n0, n1, direct, part, total, own_norm, near, far, image, stack, norm, early,
-    in_sem, sent, tree_recv, sums_recv, norm_sent, norm_recv, d2d_recv, early_recv, here,
+    in_sem, sent, tree_recv, sums_recv, norm_recv, d2d_recv, early_recv, here,
 ):
     f, t = lax.axis_index("fsdp"), lax.axis_index("tp")
     y, p, c = f // 4, (f // 2) % 2, f % 2
@@ -69,7 +69,7 @@
 
     serve, scale = (serve_g, serve_u), (scale_g, scale_u)
     pairs = ((wg, whole_g), (fg, a1), (sg, a2), (wu, whole_u), (fu, b1), (su, b2), (nt, n0), (ns, n1))
-    loads = [pltpu.make_async_copy(src, dst, in_sem.at[i]) for i, (src, dst) in enumerate(pairs)]
+    loads = [pltpu.make_async_copy(src, dst, in_sem.at[i // 3]) for i, (src, dst) in enumerate(pairs)]
     for load in loads:
         load.start()
 
@@ -87,9 +87,9 @@
         else:
             part[row] = sums
 
-    def share(slots, slot, recv, to, send=None):
+    def share(slots, slot, recv, to):
         for q in to:
-            remote(slots.at[slot], slots.at[slot], sent.at[2] if send is None else send, recv, q).start()
+            remote(slots.at[slot], slots.at[slot], sent.at[2], recv, q).start()
 
     def wait_slots(slots, n, sem):
         pltpu.make_async_copy(slots.at[pl.ds(0, n)], slots.at[pl.ds(0, n)], sem).wait()
@@ -97,7 +97,8 @@
     def leave_early(i):
         r, n, s, _ = UNITS[0][EARLY[i]]
         for k, q in enumerate((at(s, 0, 0), at(-s, 0, 0), at(0, 1, 0))):
-            remote(whole_g.at[pl.ds(r, n)], early.at[k, pl.ds(EARLY_AT[i], n)], sent.at[3], early_recv.at[0], q).start()
+            src, dst = whole_g.at[pl.ds(r, n)], early.at[k, pl.ds(EARLY_AT[i], n)]
+            remote(src, dst, sent.at[3], early_recv.at[0], q).start()
 
     def narrow(g, w):
         slots, n = (direct, 15) if g == 0 else (total, 3)
@@ -134,12 +135,9 @@
     for load in loads[:3]:
         load.wait()
     update(whole_g, a1, a2, 0)
-    pl.semaphore_wait(barrier, len(peers) + z + side)
-    share(direct, f, sums_recv.at[0], peers)
     for load in loads[3:]:
         load.wait()
     update(whole_u, b1, b2, 1)
-    share(part, row, sums_recv.at[2], row_peers)
 
     own_norm[...] = jnp.zeros_like(own_norm)
     own_norm[0:1, 0:24] = (n0[...] + n1[...]).astype(jnp.bfloat16).astype(jnp.float32)
@@ -147,7 +145,11 @@
     rolled = pltpu.roll(jnp.broadcast_to(own_norm[0:1, :], (8, 128)), first % 128, 1)
     place = 128 * lax.broadcasted_iota(jnp.int32, (8, 128), 0) + lax.broadcasted_iota(jnp.int32, (8, 128), 1) - first
     near[row] = jnp.where((place >= 0) & (place < 24), rolled, 0.0)[0:2]
-    share(near, row, norm_recv.at[0], row_peers, norm_sent.at[0])
+
+    pl.semaphore_wait(barrier, len(peers) + z + side)
+    share(direct, f, sums_recv.at[0], peers)
+    share(part, row, sums_recv.at[2], row_peers)
+    share(near, row, norm_recv.at[0], row_peers)
     leave_early(0)
     leave_early(1)
     for q in tp_peers:
@@ -161,7 +163,7 @@
     share(total, y, sums_recv.at[1], ring_peers)
     wait_slots(near, 3, norm_recv.at[0])
     far[y] = near[...]
-    share(far, y, norm_recv.at[1], ring_peers, norm_sent.at[1])
+    share(far, y, norm_recv.at[1], ring_peers)
 
     inverse = narrow(0, whole_g)
     own(0)
@@ -188,7 +190,7 @@
 
     def norm_to(src, dst, k, q):
         return pltpu.make_async_remote_copy(
-            src_ref=src, dst_ref=dst, send_sem=norm_sent.at[k], recv_sem=norm_recv.at[k],
+            src_ref=src, dst_ref=dst, send_sem=sent.at[2], recv_sem=norm_recv.at[k],
             device_id=(f, q), device_id_type=MESH,
         )
 
@@ -199,11 +201,13 @@
         give(g, 0, 0)
 
     for g in (0, 1):
-        for u, (_, _, s, crossings) in enumerate(UNITS[g][:4]):
-            arrived(g, "A", u)
-            send(g, u, "D", at(-s, 0, 0), at(s, 0, 0))
-            send(g, u, "E", at(-s, 0, 0), at(0, 1, 0))
-            if crossings == 2:
+        for units in ((0,), (1,), (2, 3)):
+            arrived(g, "A", units[0])
+            for u in units:
+                s = UNITS[g][u][2]
+                send(g, u, "D", at(-s, 0, 0), at(s, 0, 0))
+                send(g, u, "E", at(-s, 0, 0), at(0, 1, 0))
+            if units[0] < 2:
                 arrived(g, "C", u)
                 send(g, u, "F", at(0, 1, 0), at(-s, 0, 0))
         arrived(g, "C", 2)
@@ -213,19 +217,20 @@
     for q in tp_peers[:3]:
         norm_to(stack.at[z], stack.at[z], 3, q).start()
     for g in (0, 1):
+        arrived(g, "B", 2)
         for u in (2, 3):
             s = UNITS[g][u][2]
-            arrived(g, "B", u)
             send(g, u, "F", at(s, 0, 0), at(0, 1, 0))
         arrived(g, "B", 0)
         give(g, 1, 0)
         give(g, 3, 0)
 
     for g in (0, 1):
-        for u in (*EARLY, 0, 1, 2, 3) if g == 0 else range(4):
-            s = UNITS[g][u][2]
-            arrived(g, "E", u)
-            send(g, u, "G", at(-s, 1, 0), at(s, 0, 0))
+        for units in (EARLY, (0,), (1,), (2, 3)) if g == 0 else ((0,), (1,), (2, 3)):
+            arrived(g, "E", units[0])
+            for u in units:
+                s = UNITS[g][u][2]
+                send(g, u, "G", at(-s, 1, 0), at(s, 0, 0))
     for g in (0, 1):
         arrived(g, "D", 0)
         give(g, 2, 0)
@@ -259,10 +264,10 @@
         (part.at[pl.ds(0, 3)], sent.at[2]),
         (total.at[pl.ds(0, 3)], sent.at[2]),
         (early, sent.at[3]),
-        (near.at[pl.ds(0, 3)], norm_sent.at[0]),
-        (far.at[pl.ds(0, 3)], norm_sent.at[1]),
-        (image.at[0], norm_sent.at[2]),
-        (stack.at[pl.ds(0, 3)], norm_sent.at[3]),
+        (near.at[pl.ds(0, 3)], sent.at[2]),
+        (far.at[pl.ds(0, 3)], sent.at[2]),
+        (image.at[0], sent.at[2]),
+        (stack.at[pl.ds(0, 3)], sent.at[2]),
     ):
         pltpu.make_async_copy(ref, ref, sem).wait()
 
@@ -311,7 +316,7 @@
             pltpu.VMEM((4, 24, 128), bf16),
             pltpu.VMEM((32, 128), f32),
             pltpu.VMEM((3, EARLY_ROWS, cols), f32),
-            dma((8,)), dma((4,)), dma((2, max(map(len, SEMAPHORES)))), dma((3,)), dma((4,)), dma((4,)), dma((2,)), dma((1,)),
+            dma((3,)), dma((4,)), dma((2, max(map(len, SEMAPHORES)))), dma((3,)), dma((4,)), dma((2,)), dma((1,)),
             pltpu.SemaphoreType.REGULAR,
         ],
         compiler_params=pltpu.CompilerParams(collective_id=0, has_side_effects=True, vmem_limit_bytes=16 * 2**20),

time: 59.4 us -> 59.1 us (level)
  no operation moved by 1% of the time
where the time goes in v5:
time: 59.1 us; the launch traced here: 59 us
  Pallas kernels  58.3 us (99%)
  between operations  0.64 us (1%)
    pallas_call x1, Pallas kernels, per_device(): pl.pallas_call(functools.partial(kernel, d_model), name='step', out_shape...  53.2 us
    pallas_call x1, Pallas kernels, per_device(): pl.pallas_call(keep, name='keep', out_shape=tuple((jax.ShapeDtypeStruct(*...  5.16 us

profile of v5, /device:TPU:1, one launch (start us, length us, event | category | flops | bytes accessed | tf_op | source)
XLA Modules:
  0.0 59.0 jit_solution(8102709994713816524)
XLA Ops:
  0.6 53.2 %step.1 = (bf16[16,192,1024]{2,1,0:T(8,128)(2,1)S(1)}, bf16[16,192,1024]{2,1,0:T(8,128)(2,1)S(1)}, f32[1,1024]{1,0:T(1,128)S(1)}, f32[1,1024]{1,0:T(1,128)S(1)},...) custom-call(f32[192,1024]{1,0:T(8,128)} %wg.1, f32[192,1024]{1,0:T(8,128)} %fg.1, ...), custom_call_target="tpu_custom_call" | custom-call | tf_op jit(solution)/shard_map/step/pallas_call | solution.py:300
  53.8 5.2 %keep.1 = (bf16[16,192,1024]{2,1,0:T(8,128)(2,1)}, bf16[16,192,1024]{2,1,0:T(8,128)(2,1)}, f32[1,1024]{1,0:T(1,128)}, f32[1,1024]{1,0:T(1,128)}, bf16[24,128]{1,...) custom-call(bf16[16,192,1024]{2,1,0:T(8,128)(2,1)S(1)} %get-tuple-element.21.refs_0_, ...), custom_call_target="tpu_custom_call" | custom-call | tf_op jit(solution)/shard_map/keep/pallas_call | solution.py:324

commit v6 on v5

--- a/solution.py
+++ b/solution.py
@@ -25,7 +25,9 @@
     three = UNITS[g][u][3] == 3
     if kind in "AE" or (kind == "C" and not three):
         return kind, u & 6 if u > 1 else u
-    return kind, 9 if kind in "BFG" and three else 8
+    if kind == "F" and three:
+        return kind, u
+    return kind, 9 if kind in "BG" and three else 8
 
 
 SEMAPHORES, TOGETHER = [], []
@@ -248,9 +250,10 @@
         give(g, 2, 1, (0, 1, *EARLY) if g == 0 else (0, 1))
         arrived(g, "F", 2)
         give(g, 1, 1, (2,))
-        give(g, 3, 1, (3,))
         arrived(g, "G", 2)
         give(g, 2, 1, (2, 3))
+        arrived(g, "F", 3)
+        give(g, 3, 1, (3,))
 
     for g in (0, 1):
         pltpu.make_async_copy(serve[g].at[pl.ds(0, 8)], serve[g].at[pl.ds(0, 8)], d2d_recv.at[g]).wait()

time: 59.1 us -> 59.1 us (level)
  no operation moved by 1% of the time
where the time goes in v6:
time: 59.1 us; the launch traced here: 59 us
  Pallas kernels  58.4 us (99%)
  between operations  0.64 us (1%)
    pallas_call x1, Pallas kernels, per_device(): pl.pallas_call(functools.partial(kernel, d_model), name='step', out_shape...  53.2 us
    pallas_call x1, Pallas kernels, per_device(): pl.pallas_call(keep, name='keep', out_shape=tuple((jax.ShapeDtypeStruct(*...  5.16 us

profile of v6, /device:TPU:1, one launch (start us, length us, event | category | flops | bytes accessed | tf_op | source)
XLA Modules:
  0.0 59.0 jit_solution(7788696507252652618)
XLA Ops:
  0.6 53.2 %step.1 = (bf16[16,192,1024]{2,1,0:T(8,128)(2,1)S(1)}, bf16[16,192,1024]{2,1,0:T(8,128)(2,1)S(1)}, f32[1,1024]{1,0:T(1,128)S(1)}, f32[1,1024]{1,0:T(1,128)S(1)},...) custom-call(f32[192,1024]{1,0:T(8,128)} %wg.1, f32[192,1024]{1,0:T(8,128)} %fg.1, ...), custom_call_target="tpu_custom_call" | custom-call | tf_op jit(solution)/shard_map/step/pallas_call | solution.py:303
  53.9 5.2 %keep.1 = (bf16[16,192,1024]{2,1,0:T(8,128)(2,1)}, bf16[16,192,1024]{2,1,0:T(8,128)(2,1)}, f32[1,1024]{1,0:T(1,128)}, f32[1,1024]{1,0:T(1,128)}, bf16[24,128]{1,...) custom-call(bf16[16,192,1024]{2,1,0:T(8,128)(2,1)S(1)} %get-tuple-element.21.refs_0_, ...), custom_call_target="tpu_custom_call" | custom-call | tf_op jit(solution)/shard_map/keep/pallas_call | solution.py:327

commit v7 on v6

--- a/solution.py
+++ b/solution.py
@@ -27,7 +27,7 @@
         return kind, u & 6 if u > 1 else u
     if kind == "F" and three:
         return kind, u
-    return kind, 9 if kind in "BG" and three else 8
+    return kind, 9 if kind == "G" and three else 8
 
 
 SEMAPHORES, TOGETHER = [], []
@@ -223,7 +223,6 @@
         for u in (2, 3):
             s = UNITS[g][u][2]
             send(g, u, "F", at(s, 0, 0), at(0, 1, 0))
-        arrived(g, "B", 0)
         give(g, 1, 0)
         give(g, 3, 0)
 
@@ -277,7 +276,7 @@
 
 def keep(*refs):
     n = len(refs) // 2
-    copies = [pltpu.make_async_copy(refs[i], refs[n + i], refs[-1].at[i]) for i in range(n)]
+    copies = [pltpu.make_async_copy(refs[i], refs[n + i], refs[-1]) for i in range(n)]
     for cp in copies:
         cp.start()
     for cp in copies:
@@ -330,7 +329,7 @@
         out_shape=tuple(jax.ShapeDtypeStruct(*shape) for shape in shapes),
         in_specs=[vmem] * 7,
         out_specs=[any_space] * 7,
-        scratch_shapes=[dma((7,))],
+        scratch_shapes=[dma],
         compiler_params=pltpu.CompilerParams(has_side_effects=True, vmem_limit_bytes=2**20),
     )(*[pltpu.with_memory_space_constraint(a, pltpu.VMEM) for a in held])
     serving_gate, serving_up, scale_gate, scale_up, norm, whole_gate, whole_up = outs

time: 59.1 us -> 59.1 us (level)
  no operation moved by 1% of the time
where the time goes in v7:
time: 59.1 us; the launch traced here: 58.9 us
  Pallas kernels  58.3 us (99%)
  between operations  0.64 us (1%)
    pallas_call x1, Pallas kernels, per_device(): pl.pallas_call(functools.partial(kernel, d_model), name='step', out_shape...  53.2 us
    pallas_call x1, Pallas kernels, per_device(): pl.pallas_call(keep, name='keep', out_shape=tuple((jax.ShapeDtypeStruct(*...  5.1 us

profile of v7, /device:TPU:1, one launch (start us, length us, event | category | flops | bytes accessed | tf_op | source)
XLA Modules:
  0.0 58.9 jit_solution(4758797448715772757)
XLA Ops:
  0.6 53.2 %step.1 = (bf16[16,192,1024]{2,1,0:T(8,128)(2,1)S(1)}, bf16[16,192,1024]{2,1,0:T(8,128)(2,1)S(1)}, f32[1,1024]{1,0:T(1,128)S(1)}, f32[1,1024]{1,0:T(1,128)S(1)},...) custom-call(f32[192,1024]{1,0:T(8,128)} %wg.1, f32[192,1024]{1,0:T(8,128)} %fg.1, ...), custom_call_target="tpu_custom_call" | custom-call | tf_op jit(solution)/shard_map/step/pallas_call | solution.py:302
  53.8 5.1 %keep.1 = (bf16[16,192,1024]{2,1,0:T(8,128)(2,1)}, bf16[16,192,1024]{2,1,0:T(8,128)(2,1)}, f32[1,1024]{1,0:T(1,128)}, f32[1,1024]{1,0:T(1,128)}, bf16[24,128]{1,...) custom-call(bf16[16,192,1024]{2,1,0:T(8,128)(2,1)S(1)} %get-tuple-element.21.refs_0_, ...), custom_call_target="tpu_custom_call" | custom-call | tf_op jit(solution)/shard_map/keep/pallas_call | solution.py:326
